TPU v7x, 32 devices: a whole 2x2x4 slice. The times are simulated.
32 devices in a mesh: slab: 16 (over z, x, core), chan: 2 (over y).
Axes of the slice: x: 2, y: 2, z: 4, core: 2. Of those that a mesh axis runs over, the one named last changes fastest.
Arguments:
- species: int32 [4096], P('slab'), may hold values from 0 to 4
- atom_count: int32 [16], P('slab'), may hold values from 192 to 256, as said below
- halo_index: int32 [16, 2, 128], P('slab'), may hold values from 0 to 255, as said below
- edge_count: int32 [16, 2], P('slab'), may hold values from 512 to 12288, as said below
- inner_edges: int32 [2, 196608], P(None, 'slab'), may hold values from 0 to 255, as said below
- outer_edges: int32 [2, 65536], P(None, 'slab'), may hold values from 0 to 255, as said below
- inner_vec: float32 [3, 196608], P(None, 'slab'), may hold values from -4.8 to 4.8, as said below
- outer_vec: float32 [3, 65536], P(None, 'slab'), may hold values from -4.8 to 4.8, as said below
- embed_table: bfloat16 [64, 5], replicated, may hold values from -6 to 6
- radial_in: bfloat16 [2, 64, 8], replicated, may hold values from -2 to 2
- radial_mid: bfloat16 [2, 64, 64], replicated, may hold values from -0.75 to 0.75
- radial_out: bfloat16 [2, 10, 64, 64], P(None, None, 'chan'), may hold values from -0.75 to 0.75
- mix_in: bfloat16 [2, 3, 64, 64], P(None, None, 'chan'), may hold values from -0.75 to 0.75
- mix_scalar: bfloat16 [2, 192, 64], replicated, may hold values from -0.75 to 0.75
- mix_irrep: bfloat16 [2, 2, 64, 64], replicated, may hold values from -0.75 to 0.75
- readout: float32 [64], replicated, may hold values from -0.75 to 0.75
- species_energy: float32 [5], replicated, may hold values from -6 to -2
Outputs:
- node_state: float32 [9, 64, 4096], P(None, None, 'slab')
- atom_energy: float32 [4096], P('slab')
- mean_energy: float32 [], replicated
Inputs may be any that keep to these rules, and one draw needn't show every extreme that they name: `atom_count`: each slab holds between 192 and 256 live atoms (rounded down), live slots first; some slab holds exactly 256. `halo_index`: every entry names a live atom of its own slab. `edge_count`: column 0 lies between 1536 and 12288, column 1 between 512 and 4096 (rounded down); live slots come first in each list; each column reaches its most in some slab. `inner_edges`: both rows name live atoms of the same slab, in every slot. `outer_edges`: row 0 lies below 256; row 1 names a live atom of the slab, in every slot. `inner_vec`: every displacement is shorter than 4.8; nearly all are 0.9 or longer, and a rare few are shorter. `outer_vec`: every displacement is shorter than 4.8; nearly all are 0.9 or longer, and a rare few are shorter.
All inputs are finite; a program needn't handle non-finite values.
Results may differ from a plain program's by a relative error of at most 0.00045.
Values may be sent and summed in bfloat16 or wider, within the bound.
A program may use at most 64 MiB of HBM per device.

v0:
```python
import functools
import math

import jax
import jax.numpy as jnp
from jax import lax
from jax.experimental import pallas as pl
from jax.experimental.pallas import tpu as pltpu
from jax.sharding import PartitionSpec as P

cutoff = 5.0
neighbour_norm = 1.0 / math.sqrt(48.0)
root_three = math.sqrt(3.0)
half_root = 0.5 * math.sqrt(3.0)
BLOCK = 2048
WIDE = 4096
f32 = jnp.float32
bf16 = jnp.bfloat16


def dot(a, b):
    return jnp.dot(a, b, preferred_element_type=f32)


def dot_nt(a, b):
    return lax.dot_general(a, b, (((1,), (1,)), ((), ())), preferred_element_type=f32)


def sigmoid(v):
    return 0.5 * jnp.tanh(0.5 * v) + 0.5


def silu(v):
    half = 0.5 * v
    return half * jnp.tanh(half) + half


def onehot_rows(index, rows):
    slots = lax.broadcasted_iota(jnp.int32, (rows, index.shape[1]), 0)
    return jnp.where(slots == index, 1.0, 0.0).astype(bf16)


def turned(matrix):
    return matrix.astype(f32).T.astype(bf16)


def initial(embed_ref, species_row):
    return dot(turned(embed_ref[...]), onehot_rows(species_row, embed_ref.shape[0]))


def unit(vec):
    x, y, z = vec[0:1], vec[1:2], vec[2:3]
    squared = x * x + y * y + z * z
    inverse = lax.rsqrt(squared + 0.25)
    return squared, inverse, x * inverse, y * inverse, z * inverse


def bessel_rows(squared, inverse, orders):
    length = jnp.sqrt(squared)
    fraction = jnp.minimum(length * (1.0 / cutoff), 1.0)
    cube = fraction * fraction * fraction
    sixth = cube * cube
    envelope = 1.0 - sixth * (28.0 - fraction * (48.0 - 21.0 * fraction))
    half = length * (0.5 * math.pi / cutoff)
    h2 = half * half
    sine = 1.0
    cosine = 1.0
    for order in range(12, 0, -2):
        sine = 1.0 - sine * h2 * (1.0 / ((order + 1) * order))
        cosine = 1.0 - cosine * h2 * (1.0 / (order * (order - 1)))
    sine = sine * half
    twice_cos = 2.0 - 4.0 * sine * sine
    first = 2.0 * sine * cosine
    scale = math.sqrt(2.0 / cutoff) * inverse * envelope
    before, now = jnp.zeros_like(first), first * scale
    rows = []
    for _ in range(orders):
        rows.append(now)
        before, now = now, twice_cos * now - before
    return jnp.concatenate(rows, axis=0)


def harmonics(x, y, z):
    return [
        root_three * x * y,
        root_three * y * z,
        0.5 * (2.0 * z * z - x * x - y * y),
        root_three * x * z,
        half_root * (x * x - y * y),
    ]


def radial(entry, mid, basis):
    hidden = silu(dot(entry, basis)).astype(bf16)
    return silu(dot(mid, hidden)).astype(bf16)


def first_kernel(
    block,
    count_ref,
    species_ref,
    halo_species_ref,
    inner_edges_ref,
    outer_edges_ref,
    inner_vec_ref,
    outer_vec_ref,
    embed_ref,
    mix_ref,
    radial_in_ref,
    radial_mid_ref,
    radial_out_ref,
    agg_ref,
    inner_basis_ref,
    outer_basis_ref,
    acc_ref,
    table_ref,
    mess_ref,
    entry_ref,
    paths_ref,
):
    chans = mix_ref.shape[2]
    atoms = species_ref.shape[1]
    for slot, ref in enumerate((species_ref, halo_species_ref)):
        init = initial(embed_ref, ref[...]).astype(bf16)
        table_ref[slot] = dot(mix_ref[0, 0], init).astype(bf16)
    acc_ref[...] = jnp.zeros_like(acc_ref)
    entry_ref[...] = turned(radial_in_ref[0])
    for k, path in enumerate((0, 3, 7)):
        paths_ref[k * chans : (k + 1) * chans] = radial_out_ref[0, path]

    def visit(slot, edges_ref, vec_ref, basis_ref, live, step):
        offset = pl.multiple_of(step * block, block)
        span = pl.ds(offset, block)
        source = onehot_rows(edges_ref[0:1, span], table_ref.shape[2])
        gathered = dot(table_ref[slot], source)
        squared, inverse, x, y, z = unit(vec_ref[:, span])
        basis = bessel_rows(squared, inverse, radial_in_ref.shape[1]).astype(bf16)
        basis_ref[:, span] = basis
        weights = dot(paths_ref[...], radial(entry_ref[...], radial_mid_ref[0], basis))
        q = harmonics(x, y, z)
        lanes = lax.broadcasted_iota(jnp.int32, (1, block), 1) + offset
        target = jnp.where(lanes < live, edges_ref[1:2, span], -1)
        by_vector = weights[chans : 2 * chans] * gathered
        by_tensor = weights[2 * chans : 3 * chans] * gathered
        mess_ref[0:chans] = (weights[0:chans] * gathered).astype(bf16)
        for k, part in enumerate((x, y, z)):
            mess_ref[(1 + k) * chans : (2 + k) * chans] = (by_vector * part).astype(bf16)
        for k, part in enumerate(q):
            mess_ref[(4 + k) * chans : (5 + k) * chans] = (by_tensor * part).astype(bf16)
        acc_ref[...] += dot_nt(mess_ref[...], onehot_rows(target, atoms))

    def run(slot, edges_ref, vec_ref, basis_ref, live):
        def body(step, carry):
            visit(slot, edges_ref, vec_ref, basis_ref, live, step)
            return carry

        lax.fori_loop(0, lax.div(live + (block - 1), block), body, 0)

    run(0, inner_edges_ref, inner_vec_ref, inner_basis_ref, count_ref[0, 0])
    run(1, outer_edges_ref, outer_vec_ref, outer_basis_ref, count_ref[0, 1])
    agg_ref[...] = (acc_ref[...] * neighbour_norm).astype(bf16)


def second_kernel(
    block,
    count_ref,
    table_ref,
    halo_table_ref,
    inner_edges_ref,
    outer_edges_ref,
    inner_vec_ref,
    outer_vec_ref,
    inner_hidden_ref,
    outer_hidden_ref,
    radial_out_ref,
    out_ref,
    acc_ref,
    weight_ref,
    source_ref,
    mess_ref,
    inner_held_ref,
    outer_held_ref,
    inner_sem,
    outer_sem,
):
    chans = table_ref.shape[0] // 9
    atoms = out_ref.shape[1]
    lists = (
        (inner_hidden_ref, inner_held_ref, inner_sem, count_ref[0, 0]),
        (outer_hidden_ref, outer_held_ref, outer_sem, count_ref[0, 1]),
    )

    def fetch(hidden_ref, held_ref, sem, step):
        span = pl.ds(pl.multiple_of(step * block, block), block)
        return pltpu.make_async_copy(hidden_ref.at[:, span], held_ref.at[:, span], sem.at[step])

    for hidden_ref, held_ref, sem, live in lists:

        def begin(step, carry, hidden_ref=hidden_ref, held_ref=held_ref, sem=sem):
            fetch(hidden_ref, held_ref, sem, step).start()
            return carry

        lax.fori_loop(0, lax.div(live + (block - 1), block), begin, 0)
    acc_ref[...] = jnp.zeros_like(acc_ref)
    paths, _, breadth = radial_out_ref.shape[1:]
    radial = radial_out_ref[1].reshape(paths * chans, breadth)

    def visit(table_ref, edges_ref, vec_ref, held, step):
        hidden_ref, held_ref, sem, live = held
        fetch(hidden_ref, held_ref, sem, step).wait()
        offset = pl.multiple_of(step * block, block)
        span = pl.ds(offset, block)
        onehot = onehot_rows(edges_ref[0:1, span], table_ref.shape[1])
        source_ref[...] = dot(table_ref[...], onehot)
        weight_ref[...] = dot(radial, held_ref[:, span])
        _, _, x_row, y_row, z_row = unit(vec_ref[:, span])
        q_rows = harmonics(x_row, y_row, z_row)
        height, width = 16, 128
        for lane in range(0, block, width):
            cols = slice(lane, lane + width)

            def wide(row):
                return jnp.broadcast_to(row[:, cols], (height, width))

            x, y, z = wide(x_row), wide(y_row), wide(z_row)
            q = [wide(row) for row in q_rows]
            hx, hy, hz = half_root * x, half_root * y, half_root * z
            for low in range(0, chans, height):

                def at(ref, k):
                    return ref[k * chans + low : k * chans + low + height, cols]

                def put(k, value):
                    mess_ref[k * chans + low : k * chans + low + height, cols] = value.astype(bf16)

                s = at(source_ref, 0)
                v = [at(source_ref, k) for k in (1, 2, 3)]
                t = [at(source_ref, k) for k in (4, 5, 6, 7, 8)]
                along = v[0] * x + v[1] * y + v[2] * z
                tq = t[0] * q[0] + t[1] * q[1] + t[2] * q[2] + t[3] * q[3] + t[4] * q[4]
                put(0, at(weight_ref, 0) * s + at(weight_ref, 1) * tq + at(weight_ref, 2) * along)
                ws = at(weight_ref, 3) * s
                w4, w5, w6 = at(weight_ref, 4), at(weight_ref, 5), at(weight_ref, 6)
                cross = [
                    v[1] * z - v[2] * y,
                    v[2] * x - v[0] * z,
                    v[0] * y - v[1] * x,
                ]
                t3 = 0.5 * t[2]
                grad = [
                    hy * t[0] - x * t3 + hz * t[3] + hx * t[4],
                    hx * t[0] + hz * t[1] - y * t3 - hy * t[4],
                    hy * t[1] + z * t[2] + hx * t[3],
                ]
                for k, part in enumerate((x, y, z)):
                    put(1 + k, ws * part + w4 * v[k] + w5 * cross[k] + w6 * grad[k])
                ws = at(weight_ref, 7) * s
                w8, w9 = at(weight_ref, 8), at(weight_ref, 9)
                sym = [
                    hy * v[0] + hx * v[1],
                    hz * v[1] + hy * v[2],
                    1.5 * v[2] * z - 0.5 * along,
                    hz * v[0] + hx * v[2],
                    hx * v[0] - hy * v[1],
                ]
                for k in range(5):
                    put(4 + k, ws * q[k] + w8 * t[k] + w9 * sym[k])
        lanes = lax.broadcasted_iota(jnp.int32, (1, block), 1) + offset
        target = jnp.where(lanes < live, edges_ref[1:2, span], -1)
        acc_ref[...] += dot_nt(mess_ref[...], onehot_rows(target, atoms))

    def run(table, edges_ref, vec_ref, held):
        def body(step, carry):
            visit(table, edges_ref, vec_ref, held, step)
            return carry

        lax.fori_loop(0, lax.div(held[3] + (block - 1), block), body, 0)

    run(table_ref, inner_edges_ref, inner_vec_ref, lists[0])
    run(halo_table_ref, outer_edges_ref, outer_vec_ref, lists[1])
    out_ref[...] = (acc_ref[...] * neighbour_norm).astype(bf16)


mesh_ids = pl.DeviceIdType.MESH


def greet(peers):
    barrier = pltpu.get_barrier_semaphore()
    for peer in peers:
        pl.semaphore_signal(barrier, inc=1, device_id=peer, device_id_type=mesh_ids)
    pl.semaphore_wait(barrier, len(peers))


def others(axis, total):
    me = lax.axis_index(axis)
    return [{axis: lax.rem(me + step, total)} for step in range(1, total)]


def beside(total):
    me = lax.axis_index("slab")
    return {"slab": lax.rem(me + total - 1, total)}, {"slab": lax.rem(me + 1, total)}


def send_halo(send_ref, land_ref, send_sem, recv_sem, total):
    copies = []
    for side, peer in enumerate(beside(total)):
        copies.append(
            pltpu.make_async_remote_copy(
                src_ref=send_ref.at[side],
                dst_ref=land_ref.at[1 - side],
                send_sem=send_sem.at[side],
                recv_sem=recv_sem.at[side],
                device_id=peer,
                device_id_type=mesh_ids,
            )
        )
    for copy in copies:
        copy.start()
    return copies


def species_kernel(slabs, species_ref, halo_ref, out_ref, send_ref, land_ref, send_sem, recv_sem):
    values = jnp.broadcast_to(species_ref[...].astype(f32), (16, species_ref.shape[1])).astype(bf16)
    for side in range(2):
        onehot = onehot_rows(halo_ref[side : side + 1], species_ref.shape[1])
        send_ref[side] = dot(values, onehot)[0:8]
    greet(beside(slabs))
    for copy in send_halo(send_ref, land_ref, send_sem, recv_sem, slabs):
        copy.wait()
    out_ref[...] = jnp.concatenate([land_ref[0, 0:1], land_ref[1, 0:1]], axis=1).astype(jnp.int32)


def exchange(agg_ref, all_ref, send_sem, recv_sem, total):
    part = agg_ref.shape[0] // 9
    me = lax.axis_index("chan")
    peers = others("chan", total)
    copies = []
    for k in range(9):
        span = slice(k * part, (k + 1) * part)
        for i, peer in enumerate(peers):
            copies.append(
                pltpu.make_async_remote_copy(
                    src_ref=agg_ref.at[span],
                    dst_ref=all_ref.at[me, span],
                    send_sem=send_sem.at[i, k],
                    recv_sem=recv_sem.at[i, k],
                    device_id=peer,
                    device_id_type=mesh_ids,
                )
            )
    for copy in copies:
        copy.start()
    all_ref[me] = agg_ref[...]

    def component(k):
        for copy in copies[k * len(peers) : (k + 1) * len(peers)]:
            copy.wait_recv()
        span = slice(k * part, (k + 1) * part)
        return jnp.concatenate([all_ref[i, span] for i in range(total)], axis=0)

    return copies, component


class Updates:
    def __init__(self, component, layer, scalar_ref, irrep_ref):
        self.component, self.layer, self.irrep = component, layer, irrep_ref
        chans = irrep_ref.shape[2]
        y = dot(turned(scalar_ref[layer]), component(0))
        self.scalar = silu(y[:chans])
        self.gates = sigmoid(y[chans : 2 * chans]), sigmoid(y[2 * chans :])

    def __getitem__(self, k):
        if k == 0:
            return self.scalar
        kind = 0 if k < 4 else 1
        return self.gates[kind] * dot(self.irrep[self.layer, kind], self.component(k))


def middle_kernel(
    slabs,
    parts,
    block,
    species_ref,
    halo_ref,
    agg_ref,
    embed_ref,
    mix_ref,
    scalar_ref,
    irrep_ref,
    inner_basis_ref,
    outer_basis_ref,
    radial_in_ref,
    radial_mid_ref,
    state_ref,
    scalars_ref,
    table_ref,
    halo_table_ref,
    inner_hidden_ref,
    outer_hidden_ref,
    inner_held_ref,
    outer_held_ref,
    out_sem,
    all_ref,
    send_ref,
    land_ref,
    agg_send,
    agg_recv,
    halo_send,
    halo_recv,
):
    part = mix_ref.shape[2]
    greet(others("chan", parts) + list(beside(slabs)))
    copies, component = exchange(agg_ref, all_ref, agg_send, agg_recv, parts)
    entry = turned(radial_in_ref[1])
    writes = []
    lists = (
        (inner_basis_ref, inner_held_ref, inner_hidden_ref),
        (outer_basis_ref, outer_held_ref, outer_hidden_ref),
    )
    for i, (basis_ref, held_ref, hidden_ref) in enumerate(lists):

        def body(step, carry, basis_ref=basis_ref, held_ref=held_ref):
            span = pl.ds(pl.multiple_of(step * block, block), block)
            held_ref[:, span] = radial(entry, radial_mid_ref[1], basis_ref[:, span])
            return carry

        lax.fori_loop(0, basis_ref.shape[1] // block, body, 0)
        writes.append(pltpu.make_async_copy(held_ref, hidden_ref, out_sem.at[i]))
    onehots = jnp.concatenate(
        [onehot_rows(halo_ref[side : side + 1], table_ref.shape[1]) for side in range(2)], axis=1
    )
    start = initial(embed_ref, species_ref[...])
    outs = Updates(component, 0, scalar_ref, irrep_ref)
    held = halo_ref.shape[1]
    for k in range(9):
        out = outs[k]
        if k == 0:
            for write in writes:
                write.start()
            out += start
            scalars_ref[...] = out
        state_ref[k] = out
        which = 0 if k == 0 else (1 if k < 4 else 2)
        span = slice(k * part, (k + 1) * part)
        mixed = dot(mix_ref[1, which], out.astype(bf16)).astype(bf16)
        table_ref[span] = mixed
        picked = dot(mixed, onehots).astype(bf16)
        for side in range(2):
            send_ref[side, span] = picked[:, side * held : (side + 1) * held]
    for copy in copies:
        copy.wait_send()
    for copy in send_halo(send_ref, land_ref, halo_send, halo_recv, slabs):
        copy.wait()
    for write in writes:
        write.wait()
    for side in range(2):
        halo_table_ref[:, side * held : (side + 1) * held] = land_ref[side]


def energy_kernel(
    slabs,
    parts,
    species_ref,
    count_ref,
    agg_ref,
    scalars_ref,
    scalar_ref,
    readout_ref,
    energy_ref,
    every_ref,
    atom_ref,
    mean_ref,
    all_ref,
    energies_ref,
    agg_send,
    agg_recv,
    energy_send,
    energy_recv,
):
    peers = others("slab", slabs)
    greet(others("chan", parts) + peers)
    copies, component = exchange(agg_ref, all_ref, agg_send, agg_recv, parts)
    chans, atoms = scalars_ref.shape
    lines = lax.broadcasted_iota(jnp.int32, (chans, chans), 0)
    across = lax.broadcasted_iota(jnp.int32, (chans, chans), 1)
    readout = jnp.sum(jnp.where(lines == across, readout_ref[...], 0.0), axis=1, keepdims=True)
    own = jnp.zeros((1, atoms), f32)
    for kind in range(energy_ref.shape[0]):
        own = jnp.where(species_ref[...] == kind, energy_ref[kind], own)
    lanes = lax.broadcasted_iota(jnp.int32, (1, atoms), 1)
    weight = turned(scalar_ref[1])[:chans]
    out = scalars_ref[...] + silu(dot(weight, component(0)))
    total = jnp.sum(out * readout, axis=0, keepdims=True) + own
    total = jnp.where(lanes < count_ref[0], total, 0.0)
    me = lax.axis_index("slab")
    energies_ref[me] = jnp.broadcast_to(
        jnp.sum(total, axis=1, keepdims=True), energies_ref.shape[1:]
    )
    atom_ref[...] = total
    part = agg_ref.shape[0] // 9
    every_ref[:, :part] = all_ref[:, :part]
    sums = [
        pltpu.make_async_remote_copy(
            src_ref=energies_ref.at[me],
            dst_ref=energies_ref.at[me],
            send_sem=energy_send.at[i],
            recv_sem=energy_recv.at[i],
            device_id=peer,
            device_id_type=mesh_ids,
        )
        for i, peer in enumerate(peers)
    ]
    for copy in sums:
        copy.start()
    for k in range(1, 9):
        component(k)
    every_ref[:, part:] = all_ref[:, part:]
    for copy in copies:
        copy.wait_send()
    for copy in sums:
        copy.wait()
    mean_ref[...] = jnp.sum(energies_ref[...], axis=0)[0:1, 0:1] * (1.0 / (atoms * slabs))


def last_kernel(
    every_ref, state_in_ref, scalar_ref, irrep_ref, atom_in_ref, mean_in_ref, state_ref, atom_ref, mean_ref
):
    part = every_ref.shape[1] // 9

    def component(k):
        span = slice(k * part, (k + 1) * part)
        return jnp.concatenate([every_ref[i, span] for i in range(every_ref.shape[0])], axis=0)

    outs = Updates(component, 1, scalar_ref, irrep_ref)
    for k in range(9):
        state_ref[k] = state_in_ref[k] + outs[k]
    atom_ref[...] = atom_in_ref[...]
    mean_ref[...] = mean_in_ref[...]


vmem = pl.BlockSpec(memory_space=pltpu.VMEM)
anywhere = pl.BlockSpec(memory_space=pl.ANY)
smem = pl.BlockSpec(memory_space=pltpu.SMEM)
params = pltpu.CompilerParams(vmem_limit_bytes=56 * 1024 * 1024)


def remote(number):
    return pltpu.CompilerParams(
        vmem_limit_bytes=56 * 1024 * 1024, collective_id=number, has_side_effects=True
    )


def local(
    species,
    atom_count,
    halo_index,
    edge_count,
    inner_edges,
    outer_edges,
    inner_vec,
    outer_vec,
    embed_table,
    radial_in,
    radial_mid,
    radial_out,
    mix_in,
    mix_scalar,
    mix_irrep,
    readout,
    species_energy,
):
    slabs = lax.axis_size("slab")
    parts = lax.axis_size("chan")
    atoms = species.shape[0]
    chans = embed_table.shape[0]
    part = mix_in.shape[2]
    breadth = radial_mid.shape[1]
    basis = radial_in.shape[2]
    paths = radial_out.shape[1]
    halo = halo_index[0]
    held = halo.shape[1]
    rows = 9 * part
    dma = pltpu.SemaphoreType.DMA
    species_row = species[None, :]
    embed = embed_table.T
    scalar = jnp.swapaxes(mix_scalar, 1, 2)
    halo_species = pl.pallas_call(
        functools.partial(species_kernel, slabs),
        out_shape=jax.ShapeDtypeStruct((1, 2 * held), jnp.int32),
        in_specs=[vmem] * 2,
        out_specs=vmem,
        scratch_shapes=[
            pltpu.VMEM((2, 8, held), f32),
            pltpu.VMEM((2, 8, held), f32),
            dma((2,)),
            dma((2,)),
        ],
        compiler_params=remote(0),
        name="halo_species",
    )(species_row, halo)
    block = math.gcd(BLOCK, math.gcd(inner_edges.shape[1], outer_edges.shape[1]))
    inner_total, outer_total = inner_edges.shape[1], outer_edges.shape[1]
    radial_turned = jnp.swapaxes(radial_in, 1, 2)
    agg, inner_basis, outer_basis = pl.pallas_call(
        functools.partial(first_kernel, block),
        out_shape=(
            jax.ShapeDtypeStruct((rows, atoms), bf16),
            jax.ShapeDtypeStruct((basis, inner_total), bf16),
            jax.ShapeDtypeStruct((basis, outer_total), bf16),
        ),
        in_specs=[smem] + [vmem] * 11,
        out_specs=(vmem, vmem, vmem),
        scratch_shapes=[
            pltpu.VMEM((rows, atoms), f32),
            pltpu.VMEM((2, part, atoms), bf16),
            pltpu.VMEM((rows, block), bf16),
            pltpu.VMEM((breadth, basis), bf16),
            pltpu.VMEM((3 * part, breadth), bf16),
        ],
        compiler_params=params,
        name="first_layer",
    )(
        edge_count,
        species_row,
        halo_species,
        inner_edges,
        outer_edges,
        inner_vec,
        outer_vec,
        embed,
        mix_in,
        radial_turned,
        radial_mid,
        radial_out,
    )
    state, scalars, table, halo_table, inner_hidden, outer_hidden = pl.pallas_call(
        functools.partial(
            middle_kernel, slabs, parts, math.gcd(WIDE, math.gcd(inner_total, outer_total))
        ),
        out_shape=(
            jax.ShapeDtypeStruct((9, chans, atoms), f32),
            jax.ShapeDtypeStruct((chans, atoms), f32),
            jax.ShapeDtypeStruct((rows, atoms), bf16),
            jax.ShapeDtypeStruct((rows, 2 * held), bf16),
            jax.ShapeDtypeStruct((breadth, inner_total), bf16),
            jax.ShapeDtypeStruct((breadth, outer_total), bf16),
        ),
        in_specs=[vmem] * 11,
        out_specs=(vmem, vmem, vmem, vmem, anywhere, anywhere),
        scratch_shapes=[
            pltpu.VMEM((breadth, inner_total), bf16),
            pltpu.VMEM((breadth, outer_total), bf16),
            dma((2,)),
            pltpu.VMEM((parts, rows, atoms), bf16),
            pltpu.VMEM((2, rows, held), bf16),
            pltpu.VMEM((2, rows, held), bf16),
            dma((parts - 1, 9)),
            dma((parts - 1, 9)),
            dma((2,)),
            dma((2,)),
        ],
        compiler_params=remote(1),
        name="middle",
    )(
        species_row,
        halo,
        agg,
        embed,
        mix_in,
        scalar,
        mix_irrep,
        inner_basis,
        outer_basis,
        radial_turned,
        radial_mid,
    )
    agg = pl.pallas_call(
        functools.partial(second_kernel, block),
        out_shape=jax.ShapeDtypeStruct((rows, atoms), bf16),
        in_specs=[smem] + [vmem] * 6 + [anywhere] * 2 + [vmem],
        out_specs=vmem,
        scratch_shapes=[
            pltpu.VMEM((rows, atoms), f32),
            pltpu.VMEM((paths * part, block), f32),
            pltpu.VMEM((rows, block), f32),
            pltpu.VMEM((rows, block), bf16),
            pltpu.VMEM((breadth, inner_total), bf16),
            pltpu.VMEM((breadth, outer_total), bf16),
            dma((inner_total // block,)),
            dma((outer_total // block,)),
        ],
        compiler_params=params,
        name="second_layer",
    )(
        edge_count,
        table,
        halo_table,
        inner_edges,
        outer_edges,
        inner_vec,
        outer_vec,
        inner_hidden,
        outer_hidden,
        radial_out,
    )
    every, atom_energy, mean_energy = pl.pallas_call(
        functools.partial(energy_kernel, slabs, parts),
        out_shape=(
            jax.ShapeDtypeStruct((parts, rows, atoms), bf16),
            jax.ShapeDtypeStruct((1, atoms), f32),
            jax.ShapeDtypeStruct((1, 1), f32),
        ),
        in_specs=[vmem, smem] + [vmem] * 4 + [smem],
        out_specs=(vmem, vmem, vmem),
        scratch_shapes=[
            pltpu.VMEM((parts, rows, atoms), bf16),
            pltpu.VMEM((slabs, 8, 128), f32),
            dma((parts - 1, 9)),
            dma((parts - 1, 9)),
            dma((slabs - 1,)),
            dma((slabs - 1,)),
        ],
        compiler_params=remote(2),
        name="energies",
    )(
        species_row,
        atom_count,
        agg,
        scalars,
        scalar,
        readout[None, :],
        species_energy,
    )
    node_state, atom_energy, mean_energy = pl.pallas_call(
        last_kernel,
        out_shape=(
            jax.ShapeDtypeStruct((9, chans, atoms), f32),
            jax.ShapeDtypeStruct((1, atoms), f32),
            jax.ShapeDtypeStruct((1, 1), f32),
        ),
        in_specs=[vmem] * 6,
        out_specs=(vmem, vmem, vmem),
        compiler_params=params,
        name="last",
    )(every, state, scalar, mix_irrep, atom_energy, mean_energy)
    return (node_state, atom_energy[0], mean_energy[0, 0])


def solution(mesh):
    return jax.shard_map(
        local,
        mesh=mesh,
        in_specs=(
            P("slab"),
            P("slab"),
            P("slab", None, None),
            P("slab", None),
            P(None, "slab"),
            P(None, "slab"),
            P(None, "slab"),
            P(None, "slab"),
            P(),
            P(),
            P(),
            P(None, None, "chan", None),
            P(None, None, "chan", None),
            P(),
            P(),
            P(),
            P(),
        ),
        out_specs=(P(None, None, "slab"), P("slab"), P()),
        check_vma=False,
    )
```

profile of v0, /device:TPU:0, one launch (start us, length us, event | category | flops | bytes accessed | tf_op | source)
XLA Modules:
  0.0 70.7 jit_solution(728542983730472591)
XLA Ops:
  0.6 8.9 %halo_species.1.halo_species_ref = s32[1,256]{1,0:T(1,128)} custom-call(s32[1,256]{1,0:T(1,128)} %bitcast.13, s32[2,128]{1,0:T(2,128)} %bitcast.19), custom_call_target="tpu_custom_call" | custom-call | tf_op jit(solution)/shard_map/halo_species/pallas_call | solution.py:587
  9.5 6.6 %first_layer.1 = (bf16[288,256]{1,0:T(8,128)(2,1)}, bf16[8,12288]{1,0:T(8,128)(2,1)}, bf16[8,4096]{1,0:T(8,128)(2,1)}) custom-call(s32[1,2]{1,0:T(1,128)} %count_ref.4, s32[1,256]{1,0:T(1,128)} %bitcast.14, s32[1,256]{1,0:T(1,128)} %halo_species.1.halo_species_ref, s32[2,12288]{1,0:T(2,128)} %inner_edges_ref.3, s32[2,4096]{1,0:T(2,128)} %outer_edges_ref.3, ...), custom_call_target="tpu_custom_call" | custom-call | tf_op jit(solution)/shard_map/first_layer/pallas_call | solution.py:604
  16.1 19.2 %middle.1 = (f32[9,64,256]{2,1,0:T(8,128)}, f32[64,256]{1,0:T(8,128)}, bf16[288,256]{1,0:T(8,128)(2,1)}, bf16[288,256]{1,0:T(8,128)(2,1)}, bf16[64,12288]{1,0:T(8,128)(2,1)}, /*index=5*/bf16[64,4096]{1,0:T(8,128)(2,1)}) custom-call(s32[1,256]{1,0:T(1,128)} %bitcast.15, s32[2,128]{1,0:T(2,128)} %bitcast.20, bf16[288,256]{1,0:T(8,128)(2,1)} %get-tuple-element.18.agg_ref, ...), custom_call_target="tpu_custom_call" | custom-call | tf_op jit(solution)/shard_map/middle/pallas_call | solution.py:636
  35.3 9.6 %second_layer.1.agg_ref = bf16[288,256]{1,0:T(8,128)(2,1)} custom-call(s32[1,2]{1,0:T(1,128)} %count_ref.4, bf16[288,256]{1,0:T(8,128)(2,1)} %get-tuple-element.21.table_ref, bf16[288,256]{1,0:T(8,128)(2,1)} %get-tuple-element.22.halo_table_ref, s32[2,12288]{1,0:T(2,128)} %inner_edges_ref.3, s32[2,4096]{1,0:T(2,128)} %outer_edges_ref.3, ...), custom_call_target="tpu_custom_call" | custom-call | tf_op jit(solution)/shard_map/second_layer/pallas_call | solution.py:677
  45.5 22.3 %energies.1 = (bf16[2,288,256]{2,1,0:T(8,128)(2,1)}, f32[1,256]{1,0:T(1,128)}, f32[1,1]{1,0:T(1,128)}) custom-call(s32[1,256]{1,0:T(1,128)} %bitcast.16, s32[1]{0:T(128)S(6)} %copy.20.count_ref, bf16[288,256]{1,0:T(8,128)(2,1)} %second_layer.1.agg_ref, f32[64,256]{1,0:T(8,128)} %get-tuple-element.25.scalars_ref, bf16[2,64,192]{2,1,0:T(8,128)(2,1)} %bitcast.9, ...), custom_call_target="tpu_custom_call" | custom-call | tf_op jit(solution)/shard_map/energies/pallas_call | solution.py:706
  67.8 2.9 %last.1 = (f32[9,64,256]{2,1,0:T(8,128)}, f32[1,256]{1,0:T(1,128)}, f32[1,1]{1,0:T(1,128)}) custom-call(bf16[2,288,256]{2,1,0:T(8,128)(2,1)} %get-tuple-element.26.every_ref, f32[9,64,256]{2,1,0:T(8,128)} %get-tuple-element.27.state_in_ref, bf16[2,64,192]{2,1,0:T(8,128)(2,1)} %bitcast.10, bf16[2,2,64,64]{3,2,1,0:T(8,128)(2,1)} %irrep_ref.3, ...), custom_call_target="tpu_custom_call" | custom-call | tf_op jit(solution)/shard_map/last/pallas_call | solution.py:734
where the time goes:
time: 71.1 us; the launch traced here: 70.7 us
  Pallas kernels  69.4 us (98%)
  between operations  1.31 us (2%)
    pallas_call x1, Pallas kernels, local(): pl.pallas_call(functools.partial(energy_kernel, slabs, parts), out_shape=...  22.3 us
    pallas_call x1, Pallas kernels, local(): pl.pallas_call(functools.partial(middle_kernel, slabs, parts, math.gcd(WI...  19.2 us
    pallas_call x1, Pallas kernels, local(): pl.pallas_call(functools.partial(second_kernel, block), out_shape=jax.Sha...  9.59 us
    pallas_call x1, Pallas kernels, local(): pl.pallas_call(functools.partial(species_kernel, slabs), out_shape=jax.Sh...  8.89 us
    pallas_call x1, Pallas kernels, local(): pl.pallas_call(functools.partial(first_kernel, block), out_shape=(jax.Sha...  6.57 us
    pallas_call x1, Pallas kernels, local(): pl.pallas_call(last_kernel, out_shape=(jax.ShapeDtypeStruct((9, chans, at...  2.93 us

commit v1 on v0

--- a/solution.py
+++ b/solution.py
@@ -14,6 +14,7 @@
 half_root = 0.5 * math.sqrt(3.0)
 BLOCK = 2048
 WIDE = 4096
+GROUPS = ((0, 1), (1, 4), (4, 9))
 f32 = jnp.float32
 bf16 = jnp.bfloat16
 
@@ -335,8 +336,8 @@
     me = lax.axis_index("chan")
     peers = others("chan", total)
     copies = []
-    for k in range(9):
-        span = slice(k * part, (k + 1) * part)
+    for k, (low, high) in enumerate(GROUPS):
+        span = slice(low * part, high * part)
         for i, peer in enumerate(peers):
             copies.append(
                 pltpu.make_async_remote_copy(
@@ -353,8 +354,10 @@
     all_ref[me] = agg_ref[...]
 
     def component(k):
-        for copy in copies[k * len(peers) : (k + 1) * len(peers)]:
-            copy.wait_recv()
+        for group, (low, high) in enumerate(GROUPS):
+            if k == low:
+                for copy in copies[group * len(peers) : (group + 1) * len(peers)]:
+                    copy.wait_recv()
         span = slice(k * part, (k + 1) * part)
         return jnp.concatenate([all_ref[i, span] for i in range(total)], axis=0)
 

time: 71.1 us -> 69.3 us (0.975)
  Pallas kernels: 69.4 us -> 67.5 us
    pallas_call x1, Pallas kernels: 22.3 us -> 11.3 us  [local(): pl.pallas_call(functools.partial(energy_kernel, slabs, parts), out_shape=...]
    pallas_call x1, Pallas kernels: 9.59 us -> 18.4 us  [local(): pl.pallas_call(functools.partial(second_kernel, block), out_shape=jax.Sha...]
    pallas_call x1, Pallas kernels: 6.57 us -> 12.1 us  [local(): pl.pallas_call(functools.partial(first_kernel, block), out_shape=(jax.Sha...]
    pallas_call x1, Pallas kernels: 19.2 us -> 13.9 us  [local(): pl.pallas_call(functools.partial(middle_kernel, slabs, parts, math.gcd(WI...]
where the time goes in v1:
time: 69.3 us; the launch traced here: 68.9 us
  Pallas kernels  67.5 us (97%)
  between operations  1.31 us (2%)
    pallas_call x1, Pallas kernels, local(): pl.pallas_call(functools.partial(second_kernel, block), out_shape=jax.Sha...  18.4 us
    pallas_call x1, Pallas kernels, local(): pl.pallas_call(functools.partial(middle_kernel, slabs, parts, math.gcd(WI...  13.9 us
    pallas_call x1, Pallas kernels, local(): pl.pallas_call(functools.partial(first_kernel, block), out_shape=(jax.Sha...  12.1 us
    pallas_call x1, Pallas kernels, local(): pl.pallas_call(functools.partial(energy_kernel, slabs, parts), out_shape=...  11.3 us
    pallas_call x1, Pallas kernels, local(): pl.pallas_call(functools.partial(species_kernel, slabs), out_shape=jax.Sh...  8.89 us
    pallas_call x1, Pallas kernels, local(): pl.pallas_call(last_kernel, out_shape=(jax.ShapeDtypeStruct((9, chans, at...  2.93 us

profile of v1, /device:TPU:0, one launch (start us, length us, event | category | flops | bytes accessed | tf_op | source)
XLA Modules:
  0.0 68.9 jit_solution(12433219956570379852)
XLA Ops:
  0.6 8.9 %halo_species.1.halo_species_ref = s32[1,256]{1,0:T(1,128)} custom-call(s32[1,256]{1,0:T(1,128)} %bitcast.13, s32[2,128]{1,0:T(2,128)} %bitcast.19), custom_call_target="tpu_custom_call" | custom-call | tf_op jit(solution)/shard_map/halo_species/pallas_call | solution.py:590
  9.5 12.1 %first_layer.1 = (bf16[288,256]{1,0:T(8,128)(2,1)}, bf16[8,12288]{1,0:T(8,128)(2,1)}, bf16[8,4096]{1,0:T(8,128)(2,1)}) custom-call(s32[1,2]{1,0:T(1,128)} %count_ref.4, s32[1,256]{1,0:T(1,128)} %bitcast.14, s32[1,256]{1,0:T(1,128)} %halo_species.1.halo_species_ref, s32[2,12288]{1,0:T(2,128)} %inner_edges_ref.3, s32[2,4096]{1,0:T(2,128)} %outer_edges_ref.3, ...), custom_call_target="tpu_custom_call" | custom-call | tf_op jit(solution)/shard_map/first_layer/pallas_call | solution.py:607
  21.6 13.9 %middle.1 = (f32[9,64,256]{2,1,0:T(8,128)}, f32[64,256]{1,0:T(8,128)}, bf16[288,256]{1,0:T(8,128)(2,1)}, bf16[288,256]{1,0:T(8,128)(2,1)}, bf16[64,12288]{1,0:T(8,128)(2,1)}, /*index=5*/bf16[64,4096]{1,0:T(8,128)(2,1)}) custom-call(s32[1,256]{1,0:T(1,128)} %bitcast.15, s32[2,128]{1,0:T(2,128)} %bitcast.20, bf16[288,256]{1,0:T(8,128)(2,1)} %get-tuple-element.18.agg_ref, ...), custom_call_target="tpu_custom_call" | custom-call | tf_op jit(solution)/shard_map/middle/pallas_call | solution.py:639
  35.5 18.4 %second_layer.1.agg_ref = bf16[288,256]{1,0:T(8,128)(2,1)} custom-call(s32[1,2]{1,0:T(1,128)} %count_ref.4, bf16[288,256]{1,0:T(8,128)(2,1)} %get-tuple-element.21.table_ref, bf16[288,256]{1,0:T(8,128)(2,1)} %get-tuple-element.22.halo_table_ref, s32[2,12288]{1,0:T(2,128)} %inner_edges_ref.3, s32[2,4096]{1,0:T(2,128)} %outer_edges_ref.3, ...), custom_call_target="tpu_custom_call" | custom-call | tf_op jit(solution)/shard_map/second_layer/pallas_call | solution.py:680
  54.6 11.3 %energies.1 = (bf16[2,288,256]{2,1,0:T(8,128)(2,1)}, f32[1,256]{1,0:T(1,128)}, f32[1,1]{1,0:T(1,128)}) custom-call(s32[1,256]{1,0:T(1,128)} %bitcast.16, s32[1]{0:T(128)S(6)} %copy.20.count_ref, bf16[288,256]{1,0:T(8,128)(2,1)} %second_layer.1.agg_ref, f32[64,256]{1,0:T(8,128)} %get-tuple-element.25.scalars_ref, bf16[2,64,192]{2,1,0:T(8,128)(2,1)} %bitcast.9, ...), custom_call_target="tpu_custom_call" | custom-call | tf_op jit(solution)/shard_map/energies/pallas_call | solution.py:709
  65.9 2.9 %last.1 = (f32[9,64,256]{2,1,0:T(8,128)}, f32[1,256]{1,0:T(1,128)}, f32[1,1]{1,0:T(1,128)}) custom-call(bf16[2,288,256]{2,1,0:T(8,128)(2,1)} %get-tuple-element.26.every_ref, f32[9,64,256]{2,1,0:T(8,128)} %get-tuple-element.27.state_in_ref, bf16[2,64,192]{2,1,0:T(8,128)(2,1)} %bitcast.10, bf16[2,2,64,64]{3,2,1,0:T(8,128)(2,1)} %irrep_ref.3, ...), custom_call_target="tpu_custom_call" | custom-call | tf_op jit(solution)/shard_map/last/pallas_call | solution.py:737
